TPU v7x, 32 devices: a whole 2x2x4 slice. The times are simulated.
32 devices in a mesh: cuts: 8 (over y, x, core), mode: 4 (over z).
Axes of the slice: x: 2, y: 2, z: 4, core: 2. Of those that a mesh axis runs over, the one named last changes fastest.
Arguments:
- stem: float32 [8, 16, 16, 32768], P('cuts', 'mode'), may hold values from -1.5 to 1.5
- left: float32 [6, 2, 512, 512], P(None, None, 'mode'), may hold values from -0.25 to 0.25
- right: float32 [512, 512], replicated, may hold values from -0.25 to 0.25
- slice_bits: int32 [8, 6], P('cuts'), may hold values from 0 to 1
- leg_order: int32 [6, 9], replicated, may hold values from 0 to 8, each once within a row
Outputs:
- amplitudes: float32 [16, 16, 32768], P(None, 'mode', 'cuts')
Inputs may be any that keep to these rules, and one draw needn't show every extreme that they name: slice_bits[s, t] is the value of branch t's cut bond in slice s. Each row of leg_order is a permutation of 0 to 8.
All inputs are finite; a program needn't handle non-finite values.
Results may differ from a plain program's by a relative error of at most 0.00018.
Values sent between devices are 32-bit elements; how exact they have to be, the bound alone decides.
No kernel may reach another device: no remote copies, remote signals or barrier semaphores. Data moves between devices by JAX's collectives and lax.ppermute only.
A program may use at most 128 MiB of HBM per device.

v0:
```python
import jax
import jax.numpy as jnp
from jax import lax
from jax.sharding import PartitionSpec as P

HIGHEST_PRECISION = lax.Precision.HIGHEST


def leg_columns(leg_map, leg_count):
    indices = jnp.arange(2**leg_count, dtype=jnp.int32)
    shifts = leg_count - 1 - leg_map
    chosen = jnp.right_shift(indices[:, None], shifts[None, :]) & 1
    powers = jnp.left_shift(
        jnp.ones((leg_count,), jnp.int32), leg_count - 1 - jnp.arange(leg_count, dtype=jnp.int32)
    )
    return jnp.sum(chosen * powers[None, :], axis=1)


def per_device(stem, left, right, slice_bits, leg_order):
    slices, leading, middle, trailing = stem.shape
    leg_count = leg_order.shape[1]
    branch_size = 2**leg_count
    total_modes = 8 + trailing.bit_length() - 1
    devices_mode = lax.axis_size("mode")
    picked = jnp.where((slice_bits == 1)[:, :, None, None], left[None, :, 1], left[None, :, 0])

    def branch_right(branch):
        return jnp.take(right, leg_columns(leg_order[branch], leg_count), axis=1)

    def build(fragment, permuted):
        count_a, count_b, width = fragment.shape
        product = jnp.dot(
            fragment.reshape(count_a * count_b, width), permuted, precision=HIGHEST_PRECISION
        )
        return product.reshape(count_a, count_b, branch_size)

    def fetch(branch, kernel):
        return kernel(
            lax.all_gather(
                build(picked[:, branch], branch_right(branch)), "mode", axis=1, tiled=True
            ),
            jnp.int32(0),
        )

    def run_absorb(tensor, first, branch):
        after = 2 ** (total_modes - first - leg_count)
        prefix = tensor.shape[1] // (branch_size * after)
        if after == 1:
            shaped = tensor.reshape(slices, prefix, branch_size)

            def kernel(fragment, offset):
                return jnp.einsum("sji,spi->spj", fragment, shaped, precision=HIGHEST_PRECISION)

        else:
            shaped = tensor.reshape(slices, prefix, branch_size, after)

            def kernel(fragment, offset):
                return jnp.einsum("sji,spir->spjr", fragment, shaped, precision=HIGHEST_PRECISION)

        return fetch(branch, kernel).reshape(slices, -1)

    tensor = stem.reshape(slices, -1)
    tensor = run_absorb(tensor, total_modes - leg_count, 0)
    tensor = run_absorb(tensor, 6, 1)
    tensor = run_absorb(tensor, 4, 2)
    columns = middle // devices_mode
    head_states = leading * devices_mode
    inner_head = 2 ** (leg_count - 4)
    head_matrix = lax.all_gather(build(picked[:, 3], branch_right(3)), "mode", axis=1, tiled=True)
    head_blocks = head_matrix.reshape(slices, head_states, inner_head, head_states, inner_head)
    blocks = tensor.reshape(
        slices, leading, devices_mode, columns, inner_head, trailing // inner_head
    )
    received = lax.all_to_all(blocks, "mode", split_axis=2, concat_axis=1, tiled=True)
    arranged = received.reshape(slices, head_states, columns, inner_head, received.shape[5])
    result = jnp.einsum("sabcd,scxdr->saxbr", head_blocks, arranged, precision=HIGHEST_PRECISION)
    tensor = result.reshape(slices, -1)
    tensor = run_absorb(tensor, total_modes - leg_count, 4)
    inner_pair = 2 ** (leg_count - 2)
    shaped_pair = tensor.reshape(slices, 4, 4, columns, inner_pair, -1)

    def pair_kernel(fragment, offset):
        pieces = fragment.reshape(slices, fragment.shape[1], 4, inner_pair)
        return jnp.einsum("sjce,sacxer->sjaxr", pieces, shaped_pair, precision=HIGHEST_PRECISION)

    result = fetch(5, pair_kernel)
    result = result.reshape(slices, 4, inner_pair, 4, columns, -1).transpose(0, 3, 1, 4, 2, 5)
    tensor = result.reshape(slices, head_states, columns, trailing)
    summed = jnp.sum(tensor, axis=0)
    return lax.psum_scatter(summed, "cuts", scatter_dimension=2, tiled=True)


def solution(mesh):
    in_specs = (
        P("cuts", "mode", None, None),
        P(None, None, "mode", None),
        P(),
        P("cuts", None),
        P(),
    )
    out_specs = P(None, "mode", "cuts")
    return jax.shard_map(
        per_device, mesh=mesh, in_specs=in_specs, out_specs=out_specs, check_vma=False
    )
```

profile of v0, /device:TPU:0, one launch (start us, length us, event | category | flops | bytes accessed | tf_op | source)
XLA Modules:
  0.0 568.8 jit_solution(1955522628350760730)
XLA Ops:
  14.5 3.2 fusion.23
  20.1 3.2 fusion.21
  25.8 3.2 fusion.18
  29.0 9.4 %reshape.121 = f32[4096,512]{1,0:T(8,128)} reshape(f32[1,4,16,32768]{3,2,1,0:T(8,128)} %param.7) | data formatting | bytes 16777216 | tf_op jit(solution)/shard_map/reshape.2
  38.4 10.2 %all-gather.15.cloned.1.call-done = f32[512,512]{1,0:T(8,128)} async-done(((f32[128,512]{1,0:T(8,128)}), f32[512,512]{1,0:T(8,128)}) %all-gather.15.cloned.1.call-update) | async-done | bytes 1048592 | tf_op jit(solution)/shard_map/all_gather | solution.py:39
  48.6 17.5 %convolution_bitcast_fusion = f32[4096,512]{0,1:T(8,128)} fusion(f32[512,512]{1,0:T(8,128)} %all-gather.15.cloned.1.call-done, f32[4096,512]{1,0:T(8,128)} %reshape.121), kind=kOutput, calls=%fused_computation.9 | convolution fusion | flops 12884901888 | bytes 17825792 | tf_op jit(solution)/shard_map/sji,spi->spj/dot_general | solution.py:52
  66.0 9.0 %copy.55 = f32[4096,512]{1,0:T(8,128)} copy(f32[4096,512]{0,1:T(8,128)} %convolution_bitcast_fusion) | data formatting | bytes 16777216 | tf_op jit(solution)/shard_map/sji,spi->spj/dot_general | solution.py:52
  75.0 9.4 %reshape.122 = f32[16,512,256]{2,1,0:T(8,128)} reshape(f32[4096,512]{1,0:T(8,128)} %copy.55) | data formatting | bytes 16777216 | tf_op jit(solution)/shard_map/reshape.6
  84.4 30.2 %convolution_bitcast_fusion.1 = f32[1,16,512,256]{2,3,1,0:T(8,128)} fusion(f32[16,512,256]{2,1,0:T(8,128)} %reshape.122, f32[512,512]{1,0:T(8,128)} %all-gather.17.cloned.1.call-done), kind=kOutput, calls=%fused_computation.14 | convolution fusion | flops 12884901888 | bytes 17825792 | tf_op jit(solution)/shard_map/sji,spir->spjr/dot_general | solution.py:58
  114.6 9.3 %copy.58 = f32[1,16,512,256]{3,2,1,0:T(8,128)} copy(f32[1,16,512,256]{2,3,1,0:T(8,128)} %convolution_bitcast_fusion.1) | data formatting | bytes 16777216 | tf_op jit(solution)/shard_map/sji,spir->spjr/transpose | solution.py:58
  123.9 9.7 %reshape.125 = f32[4,512,1024]{2,1,0:T(8,128)} reshape(f32[1,16,512,256]{3,2,1,0:T(8,128)} %copy.58) | data formatting | bytes 16777216 | tf_op jit(solution)/shard_map/reshape.9
  133.6 18.2 %fusion.16 = f32[4,1024,512]{1,2,0:T(8,128)S(1)} fusion(f32[4,512,1024]{2,1,0:T(8,128)} %reshape.125, f32[512,512]{1,0:T(8,128)} %all-gather.19.cloned.1.call-done), kind=kOutput, calls=%fused_computation.21 | convolution fusion | flops 12884901888 | bytes 17825792 | tf_op jit(solution)/shard_map/sji,spir->spjr/dot_general | solution.py:58
  151.9 4.1 copy.60
  155.9 5.6 all-to-all-start
  164.2 3.2 fusion.14
  169.9 3.2 fusion.26
  175.5 3.2 fusion.12
  178.8 57.3 %all-gather.21.cloned.1.call-done = f32[512,512]{1,0:T(8,128)} async-done(((f32[128,512]{1,0:T(8,128)}), f32[512,512]{1,0:T(8,128)}) %all-gather.21.cloned.1.call-update) | async-done | bytes 1048592 | tf_op jit(solution)/shard_map/all_gather | solution.py:69
  236.1 3.8 reshape.130
  239.9 37.6 %all-gather.13.cloned.1.call-done = f32[512,512]{1,0:T(8,128)} async-done(((f32[128,512]{1,0:T(8,128)}), f32[512,512]{1,0:T(8,128)}) %all-gather.13.cloned.1.call-update) | async-done | bytes 1048592 | tf_op jit(solution)/shard_map/all_gather | solution.py:39
  279.1 115.9 %all-to-all-done = f32[1,4,4,4,32,1024]{5,4,3,1,0,2:T(8,128)} async-done(((f32[1,4,4,4,32,1024]{5,4,3,1,0,2:T(8,128)}), f32[1,4,4,4,32,1024]{5,4,3,1,0,2:T(8,128)}, u32[]{:S(2)}, u32[]{:S(2)}) %all-to-all-start) | async-done | bytes 8388640 | tf_op jit(solution)/shard_map/all_to_all | solution.py:74
  395.0 4.4 copy.61
  399.6 18.9 %fusion.9 = f32[1,16,4,32,1024]{4,3,1,2,0:T(8,128)S(1)} fusion(f32[16,4,32,1024,1]{3,2,0,4,1:T(8,128)S(1)} %bitcast.122, f32[16,32,16,32]{3,2,1,0:T(8,128)S(1)} %copy-done), kind=kOutput, calls=%fused_computation.15 | convolution fusion | flops 12884901888 | bytes 17825792 | tf_op jit(solution)/shard_map/sabcd,scxdr->saxbr/dot_general | solution.py:76
  418.6 4.1 copy.64
  422.6 9.4 %reshape.131 = f32[4096,512]{1,0:T(8,128)} reshape(f32[1,16,4,32,1024]{4,3,2,1,0:T(8,128)} %copy.64) | data formatting | bytes 16777216 | tf_op jit(solution)/shard_map/reshape.27
  432.0 17.7 %fusion.52 = f32[4096,512]{1,0:T(8,128)} fusion(f32[4096,512]{1,0:T(8,128)} %reshape.131, f32[512,512]{1,0:T(8,128)} %all-gather.23.cloned.1.call-done), kind=kOutput, calls=%fused_computation.95 | convolution fusion | flops 12884901888 | bytes 17825792 | tf_op jit(solution)/shard_map/sji,spi->spj/dot_general | solution.py:52
  449.7 9.4 %reshape.134 = f32[4,4,4,128,256]{4,3,2,1,0:T(8,128)} reshape(f32[4096,512]{1,0:T(8,128)} %fusion.52) | data formatting | bytes 16777216 | tf_op jit(solution)/shard_map/reshape.32
  459.0 16.0 %fusion.6 = f32[1,4,4,4,128,256]{5,4,3,1,2,0:T(8,128)S(1)} fusion(f32[4,4,4,128,256]{4,3,2,1,0:T(8,128)} %reshape.134, f32[4,128,4,128,1,1]{3,2,1,0,5,4:T(4,128)S(1)} %bitcast.123), kind=kOutput, calls=%fused_computation.13 | convolution fusion | flops 12884901888 | bytes 17825792 | tf_op jit(solution)/shard_map/sjce,sacxer->sjaxr/dot_general | solution.py:84
  475.0 3.8 copy.68
  478.8 9.4 %reduce_sum.66 = f32[16,4,32768]{2,0,1:T(8,128)} reshape(f32[1,4,4,4,128,256]{5,4,2,1,3,0:T(8,128)} %copy.68) | data formatting | bytes 16777216 | tf_op jit(solution)/shard_map/reduce_sum | solution.py:89
  488.2 70.5 %reduce-scatter.2.cloned.1.call-done = f32[16,4,4096]{2,0,1:T(8,128)} async-done(((f32[16,4,32768]{2,0,1:T(8,128)}), f32[16,4,4096]{2,0,1:T(8,128)}) %reduce-scatter.2.cloned.1.call-update) | async-done | bytes 1048592 | tf_op jit(solution)/shard_map/reduce_scatter | solution.py:90
  558.7 2.9 copy.69
  (50 shorter events, 21.9 us)
Async XLA Ops:
  6.5 42.0 %all-gather.15.cloned.1.call-start = ((), (), s32[]{:S(2)}) async-start(), calls=%async_computation.4 | async-start | bytes 1310720 | tf_op jit(solution)/shard_map/all_gather | solution.py:39
  17.7 66.7 %all-gather.17.cloned.1.call-start = ((), (), s32[]{:S(2)}) async-start(), calls=%async_computation.5 | async-start | bytes 1310720 | tf_op jit(solution)/shard_map/all_gather | solution.py:39
  23.3 110.3 %all-gather.19.cloned.1.call-start = ((), (), s32[]{:S(2)}) async-start(), calls=%async_computation.6 | async-start | bytes 1310720 | tf_op jit(solution)/shard_map/all_gather | solution.py:39
  155.9 239.1 %all-to-all-start = ((f32[1,4,4,4,32,1024]{5,4,3,1,0,2:T(8,128)}), f32[1,4,4,4,32,1024]{5,4,3,1,0,2:T(8,128)}, u32[]{:S(2)}, u32[]{:S(2)}) async-start(f32[1,4,4,4,32,1024]{5,4,3,1,0,2:T(8,128)} %copy.60), calls=%async_computation | async-start | bytes 16777216 | tf_op jit(solution)/shard_map/all_to_all | solution.py:74
  161.6 74.5 %all-gather.21.cloned.1.call-start = ((), (), s32[]{:S(2)}) async-start(), calls=%async_computation.7 | async-start | bytes 1310720 | tf_op jit(solution)/shard_map/all_gather | solution.py:69
  167.4 110.1 %all-gather.13.cloned.1.call-start = ((), (), s32[]{:S(2)}) async-start(), calls=%async_computation.3 | async-start | bytes 1310720 | tf_op jit(solution)/shard_map/all_gather | solution.py:39
  173.1 258.9 %all-gather.23.cloned.1.call-start = ((), (), s32[]{:S(2)}) async-start(), calls=%async_computation.8 | async-start | bytes 1310720 | tf_op jit(solution)/shard_map/all_gather | solution.py:39
  178.8 379.9 %reduce-scatter.2.cloned.1.call-start = ((), (), s32[]{:S(2)}) async-start(), calls=%async_computation.2 | async-start | bytes 9437184 | tf_op jit(solution)/shard_map/reduce_scatter | solution.py:90
  395.0 4.6 copy-start
Sparse Core Ops, SparseCore 0:
  17.8 30.6 all-gather.14
  50.1 27.3 all-gather.16
  79.1 27.3 all-gather.18
  167.6 68.5 all-gather.20
  237.5 39.9 all-gather.12
  279.0 100.0 all-gather.22
  488.3 70.3 reduce-scatter.1
where the time goes:
time: 578 us; the launch traced here: 569 us
  waiting for transfers between devices  292 us (51%)
  matrix products  138 us (24%)
  local copies, waits for them, and re-layouts  115 us (20%)
  between operations  14.1 us (2%)
  starting transfers between devices  5.9 us (1%)
    all_to_all x1, waiting for transfers between devices, per_device(): lax.all_to_all(blocks, 'mode', split_axis=2, concat_axis=1, tiled=True)  116 us
    reduce_scatter x1, waiting for transfers between devices, per_device(): return lax.psum_scatter(summed, 'cuts', scatter_dimension=2, tiled=True)  70.5 us
    all_gather x1, waiting for transfers between devices, per_device(): lax.all_gather(build(picked[:, 3], branch_right(3)), 'mode', axis=1, tile...  57.3 us
    another operation x7, local copies, waits for them, and re-layouts  52.6 us
    dot_general x2, matrix products, kernel(): jnp.einsum('sji,spir->spjr', fragment, shaped, precision=HIGHEST_PRECISION)  48.5 us
    all_gather x5, waiting for transfers between devices, fetch(): lax.all_gather(build(picked[:, branch], branch_right(branch)), 'mode', ax...  47.8 us
    dot_general x2, matrix products, kernel(): jnp.einsum('sji,spi->spj', fragment, shaped, precision=HIGHEST_PRECISION)  35.2 us
    dot_general x6, matrix products, build(): jnp.dot(fragment.reshape(count_a * count_b, width), permuted, precision=H...  19.3 us
  transfers between devices with their start and end apart: 8, of which 5 were waited for; matrix products, arithmetic and copies ran while one was open for 29% of the time, Pallas kernels for 0%

commit v1 on v0

v1 whole, which is shorter than its diff:
```python
import functools

import jax
import jax.numpy as jnp
from jax import lax
from jax.experimental import pallas as pl
from jax.experimental.pallas import tpu as pltpu
from jax.sharding import PartitionSpec as P


BF16 = jnp.bfloat16
F32 = jnp.float32
VMEM_LIMIT = 60 * 1024 * 1024


def leg_columns(leg_map, leg_count, indices):
    shifts = leg_count - 1 - leg_map
    chosen = jnp.right_shift(indices[:, None], shifts[None, :]) & 1
    powers = jnp.left_shift(
        jnp.ones((leg_count,), jnp.int32), leg_count - 1 - jnp.arange(leg_count, dtype=jnp.int32)
    )
    return jnp.sum(chosen * powers[None, :], axis=1)


def halves(value):
    high = value.astype(BF16)
    return high, (value - high.astype(F32)).astype(BF16)


def dot(a, b, contract=((1,), (0,))):
    return lax.dot_general(a, b, (contract, ((), ())), preferred_element_type=F32)


def product(a, b, contract=((1,), (0,))):
    return dot(a[0], b[0], contract) + (dot(a[0], b[1], contract) + dot(a[1], b[0], contract))


def order_kernel(columns_ref, right_ref, high_ref, low_ref):
    size = right_ref.shape[0]
    picks = lax.broadcasted_iota(jnp.int32, (size, size), 0) == columns_ref[0]
    chosen = jnp.where(picks, 1.0, 0.0).astype(BF16)
    high, low = halves(right_ref[...])
    high_ref[0] = dot(high, chosen).astype(BF16)
    low_ref[0] = dot(low, chosen).astype(BF16)


def order(right, columns):
    count, _, size = columns.shape
    block = pl.BlockSpec((1, size, size), lambda t: (t, 0, 0))
    return pl.pallas_call(
        order_kernel,
        grid=(count,),
        in_specs=[
            pl.BlockSpec((1, 1, size), lambda t: (t, 0, 0)),
            pl.BlockSpec((size, size), lambda t: (0, 0)),
        ],
        out_specs=[block] * 2,
        out_shape=[jax.ShapeDtypeStruct((count, size, size), BF16)] * 2,
        compiler_params=pltpu.CompilerParams(vmem_limit_bytes=VMEM_LIMIT),
        cost_estimate=pl.CostEstimate(
            flops=4 * count * size * size * size, bytes_accessed=4 * count * size * size, transcendentals=0
        ),
        name="order",
    )(columns, right)


def build_kernel(bits_ref, *refs):
    own_ref, (right_high, right_low, place_ref, high_ref, low_ref) = refs[:-5], refs[-5:]
    flat = lambda value: value.reshape(-1, value.shape[-1])
    left = halves(jnp.concatenate([flat(ref[:, 0, 0]) for ref in own_ref], axis=0))
    high, low = halves(product(left, (right_high[0], right_low[0])))
    size = high.shape[0]
    picks = lax.broadcasted_iota(jnp.int32, (size, size), 1) == place_ref[0]
    chosen = jnp.where(picks, 1.0, 0.0).astype(BF16)
    high_ref[0] = dot(chosen, high).astype(BF16)
    low_ref[0] = dot(chosen, low).astype(BF16)


def build(rows, starts, bits, rights, branch, wide, places):
    count, size, _ = places.shape
    width = rights[0].shape[1]
    shape = (count, size, wide)
    return pl.pallas_call(
        build_kernel,
        grid_spec=pltpu.PrefetchScalarGridSpec(
            num_scalar_prefetch=1,
            grid=(count,),
            in_specs=[
                pl.BlockSpec(
                    (value.shape[0], 1, 1) + value.shape[3:],
                    functools.partial(lambda start, t, bits: (0, t + start, bits[t], 0, 0), start),
                )
                for value, start in zip(rows, starts)
            ]
            + [pl.BlockSpec((1, width, wide), lambda t, bits: (t + branch, 0, 0))] * 2
            + [pl.BlockSpec((1, size, 1), lambda t, bits: (t, 0, 0))],
            out_specs=[pl.BlockSpec((1, size, wide), lambda t, bits: (t, 0, 0))] * 2,
        ),
        out_shape=[jax.ShapeDtypeStruct(shape, BF16)] * 2,
        compiler_params=pltpu.CompilerParams(vmem_limit_bytes=VMEM_LIMIT),
        cost_estimate=pl.CostEstimate(
            flops=10 * count * size * size * wide, bytes_accessed=8 * count * size * size, transcendentals=0
        ),
        name="build",
    )(bits, *rows, *rights, places)


def first_kernel(layout, x_ref, *refs):
    chunks, parts, inner = layout
    b0, b1, b2 = [(refs[0].at[t], refs[1].at[t]) for t in range(3)]
    outs, (high_ref, low_ref) = refs[2:-2], refs[-2:]
    size = b1[0].shape[0]
    half, quarter = size // 2, size // 4

    def lead(m4, carry):
        rows = jnp.concatenate(
            [
                x_ref[0, 0, pl.ds(pl.multiple_of(8 * m4, 8), 8), size * m : size * (m + 1)]
                for m in range(x_ref.shape[3] // size)
            ],
            axis=0,
        )
        index = lax.broadcasted_iota(jnp.int32, rows.shape, 0)
        eight, four = (index >> 3) & 1, (index >> 2) & 1
        rows = jnp.where(
            eight == four,
            rows,
            jnp.where(eight == 0, pltpu.roll(rows, rows.shape[0] - 4, 0), pltpu.roll(rows, 4, 0)),
        )
        value = product(halves(rows), (b0[0][...], b0[1][...]), ((1,), (1,)))
        value = value.reshape(half // 8, 2, 8, size)
        for m5 in range(2):
            part = value[:, m5].reshape(half, size)
            stacked = jnp.concatenate([part[:, :half], part[:, half:]], axis=0)
            result = product((b1[0][...], b1[1][...]), halves(stacked))
            high, low = halves(jnp.concatenate([result[:half], result[half:]], axis=1))
            place = pl.ds(pl.multiple_of((2 * m4 + m5) * quarter, quarter), quarter)
            for m13 in range(2):
                high_ref[m13, place, :] = high[m13 * quarter : (m13 + 1) * quarter]
                low_ref[m13, place, :] = low[m13 * quarter : (m13 + 1) * quarter]
        return carry

    lax.fori_loop(0, 2, lead, 0)

    def last(m13, carry):
        result = product((b2[0][...], b2[1][...]), (high_ref[m13], low_ref[m13]))
        for c, blocks in enumerate(chunks):
            for d in range(parts):
                for r, block in enumerate(blocks):
                    start = (block[0] * parts * inner + d * inner + block[1]) * (size // 16)
                    outs[c * parts + d][0, r, m13] = result[start : start + size // 16]
        return carry

    lax.fori_loop(0, 2, last, 0)


def first(stem, start, count, chunks, parts, inner, matrices):
    size = matrices[0].shape[1]
    trailing = stem.shape[3]
    lanes = size
    block = lambda c: (count, len(chunks[c]), 2, size // 16, lanes)
    whole = pl.BlockSpec((3, size, size), lambda k: (0, 0, 0))
    return pl.pallas_call(
        functools.partial(first_kernel, (chunks, parts, inner)),
        grid=(count,),
        in_specs=[pl.BlockSpec((1, 1, 16, trailing), lambda k: (0, k + start, 0, 0))] + [whole] * 2,
        out_specs=[
            pl.BlockSpec((1,) + block(c)[1:], lambda k: (k, 0, 0, 0, 0))
            for c in range(len(chunks))
            for _ in range(parts)
        ],
        out_shape=[
            jax.ShapeDtypeStruct(block(c), F32) for c in range(len(chunks)) for _ in range(parts)
        ],
        scratch_shapes=[pltpu.VMEM((2, size, size), BF16)] * 2,
        compiler_params=pltpu.CompilerParams(vmem_limit_bytes=VMEM_LIMIT),
        cost_estimate=pl.CostEstimate(
            flops=3 * 3 * 2 * count * 16 * trailing * size,
            bytes_accessed=8 * count * 16 * trailing,
            transcendentals=0,
        ),
        name="first",
    )(stem, *matrices)


def second_kernel(sources, pair_high, pair_low, b3h, b3l, *refs):
    inputs, (keep_ref, send_ref, high_ref, low_ref) = refs[:sources], refs[-4:]
    b4h, b5h, b4l, b5l = pair_high.at[0], pair_high.at[1], pair_low.at[0], pair_low.at[1]
    size = b5h.shape[0]
    half, quarter = size // 2, size // 4

    def head(m13, carry):
        rows = jnp.concatenate(
            [ref[k, 0, m13] for ref in inputs for k in range(ref.shape[0])], axis=0
        )
        rows = product(halves(rows), (b4h[...], b4l[...]), ((1,), (1,)))
        high, low = halves(product((b3h[0], b3l[0]), halves(rows)))
        high_ref[m13] = high
        low_ref[m13] = low
        return carry

    lax.fori_loop(0, 2, head, 0)
    states, _, depth, _ = keep_ref.shape[1:]

    def pair(lead, carry):
        place = pl.ds(pl.multiple_of(lead * quarter, quarter), quarter)
        stack = lambda ref: jnp.concatenate(
            [
                ref[m13, place, m14 * half : (m14 + 1) * half]
                for m13 in range(2)
                for m14 in range(2)
            ],
            axis=0,
        )
        result = product((b5h[...], b5l[...]), (stack(high_ref), stack(low_ref)))
        for q in range(states):
            keep_ref[0, q, lead] = result[q * depth : (q + 1) * depth]
            send_ref[0, q, lead] = result[(states + q) * depth : (states + q + 1) * depth]
        return carry

    lax.fori_loop(0, 4, pair, 0)


def second(inputs, matrices, devices_cuts):
    size = matrices[0].shape[1]
    rounds = inputs[0].shape[1]
    whole = lambda matrix: pl.BlockSpec(matrix.shape, lambda r: (0, 0, 0))
    shape = (rounds, devices_cuts // 2, 4, size // devices_cuts, size // 2)
    return pl.pallas_call(
        functools.partial(second_kernel, len(inputs)),
        grid=(rounds,),
        in_specs=[whole(matrix) for matrix in matrices]
        + [
            pl.BlockSpec((value.shape[0], 1) + value.shape[2:], lambda r: (0, r, 0, 0, 0))
            for value in inputs
        ],
        out_specs=[pl.BlockSpec((1,) + shape[1:], lambda r: (r, 0, 0, 0, 0))] * 2,
        out_shape=[jax.ShapeDtypeStruct(shape, F32)] * 2,
        scratch_shapes=[pltpu.VMEM((2, size, size), BF16)] * 2,
        compiler_params=pltpu.CompilerParams(vmem_limit_bytes=VMEM_LIMIT),
        cost_estimate=pl.CostEstimate(
            flops=3 * 2 * rounds * 4 * size * size * size,
            bytes_accessed=6 * rounds * size * size * 4,
            transcendentals=0,
        ),
        name="second",
    )(*matrices, *inputs)


def swap(value, axis, bit):
    count = lax.axis_size(axis)
    return lax.ppermute(value, axis, [(i, i ^ bit) for i in range(count)])


def scatter_sum(parts, at, descending):
    bits = parts[0].shape[1].bit_length() - 1
    arrays = [part.reshape(part.shape[:1] + (2,) * bits + part.shape[2:])[at] for part in parts]
    more, left = [], list(range(bits))
    for bit in range(bits) if descending else reversed(range(bits)):
        axis = left.index(bit)
        left.pop(axis)
        pick = lambda array, place: lax.index_in_dim(array, place, axis, keepdims=False)
        sent = functools.reduce(jnp.add, [pick(array, 1) for array in arrays])
        more.append(swap(sent, "cuts", 2 ** (bits - bit)))
        arrays = [pick(array, 0) for array in arrays] + more[-1:]
    return [(array, ()) for array in more]


def finish_kernel(inner, counts, *refs):
    refs, out_ref = list(refs[:-1]), refs[-1]
    states = out_ref.shape[0]
    for r in range(inner):
        terms = [refs.pop(0) for _ in range(counts[r])]
        total = functools.reduce(
            jnp.add, [ref[...].reshape(ref.shape[-2], ref.shape[-1]) for ref in terms]
        )
        rows, lanes = total.shape
        for row in range(rows):
            start = row % (rows // states) * lanes
            out_ref[row // (rows // states), r : r + 1, start : start + lanes] = total[row : row + 1]


def finish(terms, shape):
    flat = [term for block in terms for term in block]
    quarter = (shape[0] // 4,) + shape[1:]

    def spec(array, lead):
        front = array.ndim - 3 - len(lead)
        block = (1,) * (array.ndim - 2) + array.shape[-2:]
        return pl.BlockSpec(block, lambda a: tuple(lead) + (0,) * front + (a, 0, 0))

    return pl.pallas_call(
        functools.partial(finish_kernel, len(terms), [len(block) for block in terms]),
        grid=(4,),
        in_specs=[spec(array, lead) for array, lead in flat],
        out_specs=pl.BlockSpec(quarter, lambda a: (a, 0, 0)),
        out_shape=jax.ShapeDtypeStruct(shape, F32),
        compiler_params=pltpu.CompilerParams(vmem_limit_bytes=VMEM_LIMIT),
        name="finish",
    )(*[array for array, _ in flat])


def gather_rows(left, start, count, share):
    devices_mode, devices_cuts = lax.axis_size("mode"), lax.axis_size("cuts")
    own = left[start : start + count]
    piece = lax.dynamic_slice_in_dim(own, lax.axis_index("cuts") * share, share, 2)
    held = jnp.stack([swap(piece, "mode", d) for d in range(1, devices_mode)])
    near = [held] + [swap(held, "cuts", 2 * d) for d in range(1, devices_cuts // 2)]
    return near + [swap(value, "cuts", 1) for value in near]


def per_device(stem, left, right, slice_bits, leg_order):
    _, leading, _, trailing = stem.shape
    leg_count = leg_order.shape[1]
    size = 2**leg_count
    devices_mode, devices_cuts = lax.axis_size("mode"), lax.axis_size("cuts")
    mode, cut = lax.axis_index("mode"), lax.axis_index("cuts")
    parts = devices_mode // 2
    inner = 16 // devices_mode
    sixteenth = size // 16
    low = mode % parts
    n = jnp.arange(size, dtype=jnp.int32)

    depth = left.shape[2]
    share = depth // devices_cuts
    direct = direct_rows(depth, devices_cuts)
    if direct:
        early_rows = [left] + gather_rows(left, 0, 3, share)
        late_rows = [left] + gather_rows(left, 3, 3, share)
        early_rows[0] = late_rows[0] = left[None]
        starts = lambda first, offset: [first] + [offset] * (len(early_rows) - 1)
    else:
        early_rows, late_rows = ([lax.all_gather(left[s : s + 3], "mode")] for s in (0, 3))
        starts = lambda first, offset: [offset]

    def position(row):
        if not direct:
            return row
        far, near = (row // depth) ^ mode, (row % depth // share) ^ cut
        slot = (near % 2) * (devices_cuts // 2) + near // 2
        return jnp.where(
            far == 0,
            row % depth,
            depth + (slot * (devices_mode - 1) + far - 1) * share + row % share,
        )

    bit = lambda value, place: (value >> place) & 1
    columns_1 = bit(n, 1) * 256 + bit(n, 0) * 128 + (n >> 3 & 31) * 4 + bit(n, 2) * 2 + bit(n, 8)
    rows_1 = (n & 127) * 4 + bit(n, 7) * 2 + bit(n, 8)
    rows_2 = (((n // sixteenth) ^ (mode * inner)) * sixteenth) + n % sixteenth
    h = jnp.arange(size // 2, dtype=jnp.int32)
    local = h // sixteenth
    source = (local // leading) ^ low
    columns_3 = (
        (mode // parts) * (size // 2)
        + (source * leading + local % leading) * sixteenth
        + h % sixteenth
    )
    columns_5 = (n & 127) * 4 + (n >> 7)
    run = size // 4 // devices_cuts
    place = n // (size // devices_cuts)
    relative = (place % (devices_cuts // 2)) * 2 + place // (devices_cuts // 2)
    rest = n % (size // devices_cuts)
    rows_5 = (rest // run) * (size // 4) + (relative ^ cut) * run + rest % run
    columns = (n, columns_1, n, jnp.concatenate([columns_3, columns_3]), n, columns_5)
    rows = (n, rows_1, rows_2, n, n, rows_5)
    chosen = [leg_columns(leg_order[t], leg_count, columns[t]) for t in range(6)]
    rights = order(right, jnp.stack(chosen)[:, None, :])

    def matrices(branches, gathered, first, wide):
        places = jnp.stack([position(rows[t]) for t in branches])[:, :, None]
        bits = slice_bits[0, branches[0] : branches[-1] + 1]
        at = branches[0]
        return build(gathered, starts(at, at - first), bits, rights, at, wide, places)

    chunks, calls = plan(devices_mode)
    early = matrices((0, 1, 2), early_rows, 0, size)
    pieces = []
    for call in range(calls):
        per_call = leading // calls
        pieces.append(first(stem, call * per_call, per_call, chunks, parts, inner, early))
    arrived = [
        [
            pieces[call][c * parts + d]
            if d == 0
            else swap(pieces[call][c * parts + d], "mode", d)
            for d in range(parts)
            for call in range(calls)
        ]
        for c in range(len(chunks))
    ]
    late = [*matrices((4, 5), late_rows, 3, size), *matrices((3,), late_rows, 3, size // 2)]
    terms, far = {}, {}
    for c, blocks in enumerate(chunks):
        keep, send = second(arrived[c], late, devices_cuts)
        received = swap(send, "cuts", 1)
        for r, block in enumerate(blocks):
            more = scatter_sum((keep, received), r, block[1] % 2 == 0)
            terms[block] = [(keep, (r,)), (received, (r,))] + more
        if blocks[0][0] == 1:
            sums = [
                functools.reduce(jnp.add, [own(array, lead) for array, lead in terms[block]])
                for block in blocks
            ]
            arrival = swap(jnp.stack(sums), "mode", parts)
            far.update({block[1]: (arrival, (r,)) for r, block in enumerate(blocks)})
    summed = [terms[(0, r)] + [far[r]] for r in range(inner)]
    shape = (leading * devices_mode, inner, trailing // devices_cuts)
    return finish(summed, shape)


def own(array, lead):
    return array[tuple(lead) + (0,) * (array.ndim - 3 - len(lead))]


def direct_rows(depth, devices_cuts):
    return depth % (8 * devices_cuts) == 0


def plan(devices_mode):
    inner = 16 // devices_mode
    group = max(inner // 2, 1)
    chunks = tuple(
        tuple((m4, r) for r in range(start, start + group))
        for m4 in (1, 0)
        for start in range(0, inner, group)
    )
    return chunks, 2 if inner % 2 == 0 else 1


def solution(mesh):
    in_specs = (
        P("cuts", "mode", None, None),
        P(None, None, "mode", None),
        P(),
        P("cuts", None),
        P(),
    )
    out_specs = P(None, "mode", "cuts")

    return jax.shard_map(
        per_device, mesh=mesh, in_specs=in_specs, out_specs=out_specs, check_vma=False
    )
```

time: 578 us -> 370 us (0.64); the launches traced: 569 us -> 370 us
  matrix products: 138 us -> 0 us
  waiting for transfers between devices: 292 us -> 169 us
  Pallas kernels: 0 us -> 114 us
  local copies, waits for them, and re-layouts: 115 us -> 19.1 us
  starting transfers between devices: 5.9 us -> 56.4 us
  between operations: 14.1 us -> 0.77 us
  other arithmetic: 4.1 us -> 10.5 us
    ppermute x0 -> x50, waiting for transfers between devices: none -> 169 us  [swap(): return lax.ppermute(value, axis, [(i, i ^ bit) for i in range(count)])]
    dot_general x12 -> x0, matrix products: 138 us -> none  [the longest x2 48.5 us: kernel(): jnp.einsum('sji,spir->spjr', fragment, shaped, precision=HIGHEST_PRECISION)]
    all_to_all x1 -> x0, waiting for transfers between devices: 116 us -> none  [per_device(): lax.all_to_all(blocks, 'mode', split_axis=2, concat_axis=1, tiled=True)]
    pallas_call x0 -> x11, Pallas kernels: none -> 114 us  [the longest x4 51.1 us: second(): pl.pallas_call(functools.partial(second_kernel, len(inputs)), grid=(round...]
    all_gather x6 -> x0, waiting for transfers between devices: 105 us -> none  [the longest x1 57.3 us: per_device(): lax.all_gather(build(picked[:, 3], branch_right(3)), 'mode', axis=1, tile...]
    reduce_scatter x1 -> x0, waiting for transfers between devices: 70.5 us -> none  [per_device(): return lax.psum_scatter(summed, 'cuts', scatter_dimension=2, tiled=True)]
    another operation x8 -> x1, local copies, waits for them, and re-layouts: 56.6 us -> 0.03 us  [per_device(): rights = order(right, jnp.stack(chosen)[:, None, :])]
    ppermute x0 -> x50, starting transfers between devices: none -> 56.4 us  [swap(): return lax.ppermute(value, axis, [(i, i ^ bit) for i in range(count)])]
  transfers between devices with their start and end apart: 8 -> 50, of which waited for: 5 -> 20; matrix products, arithmetic and copies ran while one was open for 29% -> 6% of each run, Pallas kernels for 0% -> 30%
where the time goes in v1:
time: 370 us
  waiting for transfers between devices  169 us (46%)
  Pallas kernels  114 us (31%)
  starting transfers between devices  56.4 us (15%)
  local copies, waits for them, and re-layouts  19.1 us (5%)
  other arithmetic  10.5 us (3%)
    ppermute x50, waiting for transfers between devices, swap(): return lax.ppermute(value, axis, [(i, i ^ bit) for i in range(count)])  169 us
    ppermute x50, starting transfers between devices, swap(): return lax.ppermute(value, axis, [(i, i ^ bit) for i in range(count)])  56.4 us
    pallas_call x4, Pallas kernels, second(): pl.pallas_call(functools.partial(second_kernel, len(inputs)), grid=(round...  51.1 us
    pallas_call x2, Pallas kernels, first(): pl.pallas_call(functools.partial(first_kernel, (chunks, parts, inner)), g...  32.1 us
    pallas_call x3, Pallas kernels, build(): pl.pallas_call(build_kernel, grid_spec=pltpu.PrefetchScalarGridSpec(num_s...  19.5 us
  transfers between devices with their start and end apart: 50, of which 20 were waited for; matrix products, arithmetic and copies ran while one was open for 6% of the time, Pallas kernels for 30%

profile of v1, /device:TPU:0, one launch (start us, length us, event | category | flops | bytes accessed | tf_op | source)
XLA Modules:
  0.0 369.6 jit_solution(13701504997085812888)
XLA Ops:
  0.0 2.5 fusion.120
  2.5 5.1 %collective-permute-start.2 = (f32[3,2,16,512]{3,2,1,0:T(8,128)S(1)}, f32[3,2,16,512]{3,2,1,0:T(8,128)S(1)}, u32[]{:S(2)}, u32[]{:S(2)}) collective-permute-start(f32[3,2,16,512]{3,2,1,0:T(8,128)S(1)} %constant_dynamic-slice_fusion.1), channel_id=1, source_target_pairs={{0,3},{1,2},{2,1},{3,0},{4,7},{5,6},{6,5},{7,4},{8,11},{9,10},{10,... | collective-permute-start | bytes 589832 | tf_op jit(solution)/shard_map/ppermute | solution.py:252
  8.3 3.8 %collective-permute-start.12 = (f32[3,2,16,512]{3,2,1,0:T(8,128)S(1)}, f32[3,2,16,512]{3,2,1,0:T(8,128)S(1)}, u32[]{:S(2)}, u32[]{:S(2)}) collective-permute-start(f32[3,2,16,512]{3,2,1,0:T(8,128)S(1)} %constant_dynamic-slice_fusion), channel_id=1, source_target_pairs={{0,3},{1,2},{2,1},{3,0},{4,7},{5,6},{6,5},{7,4},{8,11},{9,10},{10,... | collective-permute-start | bytes 589832 | tf_op jit(solution)/shard_map/ppermute | solution.py:252
  13.5 9.0 %collective-permute-start.10 = (f32[3,2,16,512]{3,2,1,0:T(8,128)S(1)}, f32[3,2,16,512]{3,2,1,0:T(8,128)S(1)}, u32[]{:S(2)}, u32[]{:S(2)}) collective-permute-start(f32[3,2,16,512]{3,2,1,0:T(8,128)S(1)} %constant_dynamic-slice_fusion), channel_id=1, source_target_pairs={{0,1},{1,0},{2,3},{3,2},{4,5},{5,4},{6,7},{7,6},{8,9},{9,8},{10,11... | collective-permute-start | bytes 589832 | tf_op jit(solution)/shard_map/ppermute | solution.py:252
  22.5 11.2 %collective-permute-done.1 = f32[3,2,16,512]{3,2,1,0:T(8,128)S(1)} collective-permute-done((f32[3,2,16,512]{3,2,1,0:T(8,128)S(1)}, f32[3,2,16,512]{3,2,1,0:T(8,128)S(1)}, u32[]{:S(2)}, u32[]{:S(2)}) %collective-permute-start.1) | collective-permute-done | bytes 196640 | tf_op jit(solution)/shard_map/ppermute | solution.py:252
  36.8 4.3 %collective-permute-done.11 = f32[3,2,16,512]{3,2,1,0:T(8,128)S(1)} collective-permute-done((f32[3,2,16,512]{3,2,1,0:T(8,128)S(1)}, f32[3,2,16,512]{3,2,1,0:T(8,128)S(1)}, u32[]{:S(2)}, u32[]{:S(2)}) %collective-permute-start.11) | collective-permute-done | bytes 196640 | tf_op jit(solution)/shard_map/ppermute | solution.py:252
  50.0 2.4 collective-permute-start.5
  52.5 10.3 %collective-permute-done.13.refs_2_ = f32[3,3,2,16,512]{4,3,2,1,0:T(8,128)} collective-permute-done((f32[3,3,2,16,512]{4,3,2,1,0:T(8,128)S(1)}, f32[3,3,2,16,512]{4,3,2,1,0:T(8,128)}, u32[]{:S(2)}, u32[]{:S(2)}) %collective-permute-start.13) | collective-permute-done | bytes 589856 | tf_op jit(solution)/shard_map/ppermute | solution.py:252
  62.8 23.7 %collective-permute-done.14.refs_3_ = f32[3,3,2,16,512]{4,3,2,1,0:T(8,128)} collective-permute-done((f32[3,3,2,16,512]{4,3,2,1,0:T(8,128)S(1)}, f32[3,3,2,16,512]{4,3,2,1,0:T(8,128)}, u32[]{:S(2)}, u32[]{:S(2)}) %collective-permute-start.14) | collective-permute-done | bytes 589856 | tf_op jit(solution)/shard_map/ppermute | solution.py:252
  89.3 6.6 %order.1 = (bf16[6,512,512]{2,1,0:T(8,128)(2,1)}, bf16[6,512,512]{2,1,0:T(8,128)(2,1)}) custom-call(s32[6,1,512]{2,1,0:T(1,128)} %broadcast_in_dim.9.columns_ref, f32[512,512]{1,0:T(8,128)} %right_ref.1), custom_call_target="tpu_custom_call" | custom-call | flops 3221225472 | bytes 6291456 | tf_op jit(solution)/shard_map/order/pallas_call | solution.py:50
  97.1 8.4 %build.5 = (bf16[3,512,512]{2,1,0:T(8,128)(2,1)}, bf16[3,512,512]{2,1,0:T(8,128)(2,1)}) custom-call(s32[3]{0:T(128)} %slice_bitcast_fusion.20.bits_ref, f32[1,6,2,128,512]{4,3,2,1,0:T(8,128)} %bitcast.218, f32[3,3,2,16,512]{4,3,2,1,0:T(8,128)} %copy-done.10, f32[3,3,2,16,512]{4,3,2,1,0:T(8,128)} %collective-permute-done.13.refs_2_, ...), custom_call_target="tpu_custom_call" | custom-call | flops 4026531840 | bytes 6291456 | tf_op jit(solution)/shard_map/build/pallas_call | solution.py:83
  105.6 16.1 %first.2 = (f32[2,2,2,32,512]{4,3,2,1,0:T(8,128)}, f32[2,2,2,32,512]{4,3,2,1,0:T(8,128)}, f32[2,2,2,32,512]{4,3,2,1,0:T(8,128)}, f32[2,2,2,32,512]{4,3,2,1,0:T(8...) custom-call(f32[1,4,16,32768]{3,2,1,0:T(8,128)} %x_ref.3, ...), custom_call_target="tpu_custom_call" | custom-call | flops 9663676416 | bytes 8388608 | tf_op jit(solution)/shard_map/first/pallas_call | solution.py:163
  121.6 16.0 %first.3 = (f32[2,2,2,32,512]{4,3,2,1,0:T(8,128)}, f32[2,2,2,32,512]{4,3,2,1,0:T(8,128)}, f32[2,2,2,32,512]{4,3,2,1,0:T(8,128)}, f32[2,2,2,32,512]{4,3,2,1,0:T(8...) custom-call(f32[1,4,16,32768]{3,2,1,0:T(8,128)} %x_ref.3, ...), custom_call_target="tpu_custom_call" | custom-call | flops 9663676416 | bytes 8388608 | tf_op jit(solution)/shard_map/first/pallas_call | solution.py:163
  142.5 4.3 %build.4 = (bf16[1,512,256]{2,1,0:T(8,128)(2,1)}, bf16[1,512,256]{2,1,0:T(8,128)(2,1)}) custom-call(s32[1]{0:T(128)} %bitcast.18.bits_ref, f32[1,6,2,128,512]{4,3,2,1,0:T(8,128)} %bitcast.219, f32[3,3,2,16,512]{4,3,2,1,0:T(8,128)} %copy-done.2, f32[3,3,2,16,512]{4,3,2,1,0:T(8,128)} %copy-done.5, f32[3,3,2,16,512]{4,3,2,1,0:T(8,128)} %copy-done.6, ...), custom_call_target="tpu_custom_call" | custom-call | flops 671088640 | bytes 2097152 | tf_op jit(solution)/shard_map/build/pallas_call | solution.py:83
  146.8 6.8 %build.3 = (bf16[2,512,512]{2,1,0:T(8,128)(2,1)}, bf16[2,512,512]{2,1,0:T(8,128)(2,1)}) custom-call(s32[2]{0:T(128)} %slice_bitcast_fusion.21.bits_ref, f32[1,6,2,128,512]{4,3,2,1,0:T(8,128)} %bitcast.220, f32[3,3,2,16,512]{4,3,2,1,0:T(8,128)} %copy-done.2, f32[3,3,2,16,512]{4,3,2,1,0:T(8,128)} %copy-done.5, f32[3,3,2,16,512]{4,3,2,1,0:T(8,128)} %copy-done.6, ...), custom_call_target="tpu_custom_call" | custom-call | flops 2684354560 | bytes 4194304 | tf_op jit(solution)/shard_map/build/pallas_call | solution.py:83
  155.6 8.3 %collective-permute-done.21.refs_3_ = f32[2,2,2,32,512]{4,3,2,1,0:T(8,128)S(1)} collective-permute-done((f32[2,2,2,32,512]{4,3,2,1,0:T(8,128)}, f32[2,2,2,32,512]{4,3,2,1,0:T(8,128)S(1)}, u32[]{:S(2)}, u32[]{:S(2)}) %collective-permute-start.21) | collective-permute-done | bytes 524320 | tf_op jit(solution)/shard_map/ppermute | solution.py:252
  164.7 12.7 %second.4 = (f32[2,4,4,64,256]{4,3,2,1,0:T(8,128)}, f32[2,4,4,64,256]{4,3,2,1,0:T(8,128)}) custom-call(bf16[2,512,512]{2,1,0:T(8,128)(2,1)} %get-tuple-element.39.pair_high, bf16[2,512,512]{2,1,0:T(8,128)(2,1)} %get-tuple-element.40.pair_low, bf16[1,512,256]{2,1,0:T(8,128)(2,1)} %get-tuple-element.41.b3h, bf16[1,512,256]{2,1,0:T(8,128)(2,1)} %get-tuple-element.42.b3l, ...), custom_call_target="tpu_custom_call" | custom-call | flops 6442450944 | bytes 12582912 | tf_op jit(solution)/shard_map/second/pallas_call | solution.py:229
  178.7 7.8 %collective-permute-done.26.refs_3_ = f32[2,2,2,32,512]{4,3,2,1,0:T(8,128)} collective-permute-done((f32[2,2,2,32,512]{4,3,2,1,0:T(8,128)}, f32[2,2,2,32,512]{4,3,2,1,0:T(8,128)}, u32[]{:S(2)}, u32[]{:S(2)}) %collective-permute-start.26) | collective-permute-done | bytes 524320 | tf_op jit(solution)/shard_map/ppermute | solution.py:252
  186.5 12.9 %second.5 = (f32[2,4,4,64,256]{4,3,2,1,0:T(8,128)}, f32[2,4,4,64,256]{4,3,2,1,0:T(8,128)}) custom-call(bf16[2,512,512]{2,1,0:T(8,128)(2,1)} %get-tuple-element.39.pair_high, bf16[2,512,512]{2,1,0:T(8,128)(2,1)} %get-tuple-element.40.pair_low, bf16[1,512,256]{2,1,0:T(8,128)(2,1)} %get-tuple-element.41.b3h, bf16[1,512,256]{2,1,0:T(8,128)(2,1)} %get-tuple-element.42.b3l, ...), custom_call_target="tpu_custom_call" | custom-call | flops 6442450944 | bytes 12582912 | tf_op jit(solution)/shard_map/second/pallas_call | solution.py:229
  199.8 9.1 %collective-permute-done.36.refs_3_ = f32[2,2,2,32,512]{4,3,2,1,0:T(8,128)S(1)} collective-permute-done((f32[2,2,2,32,512]{4,3,2,1,0:T(8,128)S(1)}, f32[2,2,2,32,512]{4,3,2,1,0:T(8,128)S(1)}, u32[]{:S(2)}, u32[]{:S(2)}) %collective-permute-start.36) | collective-permute-done | bytes 524320 | tf_op jit(solution)/shard_map/ppermute | solution.py:252
  209.7 12.7 %second.6 = (f32[2,4,4,64,256]{4,3,2,1,0:T(8,128)}, f32[2,4,4,64,256]{4,3,2,1,0:T(8,128)}) custom-call(bf16[2,512,512]{2,1,0:T(8,128)(2,1)} %get-tuple-element.39.pair_high, bf16[2,512,512]{2,1,0:T(8,128)(2,1)} %get-tuple-element.40.pair_low, bf16[1,512,256]{2,1,0:T(8,128)(2,1)} %get-tuple-element.41.b3h, bf16[1,512,256]{2,1,0:T(8,128)(2,1)} %get-tuple-element.42.b3l, ...), custom_call_target="tpu_custom_call" | custom-call | flops 6442450944 | bytes 12582912 | tf_op jit(solution)/shard_map/second/pallas_call | solution.py:229
  222.4 8.1 %collective-permute-done.41.refs_3_ = f32[2,2,2,32,512]{4,3,2,1,0:T(8,128)S(1)} collective-permute-done((f32[2,2,2,32,512]{4,3,2,1,0:T(8,128)S(1)}, f32[2,2,2,32,512]{4,3,2,1,0:T(8,128)S(1)}, u32[]{:S(2)}, u32[]{:S(2)}) %collective-permute-start.41) | collective-permute-done | bytes 524320 | tf_op jit(solution)/shard_map/ppermute | solution.py:252
  231.3 12.8 %second.7 = (f32[2,4,4,64,256]{4,3,2,1,0:T(8,128)}, f32[2,4,4,64,256]{4,3,2,1,0:T(8,128)}) custom-call(bf16[2,512,512]{2,1,0:T(8,128)(2,1)} %get-tuple-element.39.pair_high, bf16[2,512,512]{2,1,0:T(8,128)(2,1)} %get-tuple-element.40.pair_low, bf16[1,512,256]{2,1,0:T(8,128)(2,1)} %get-tuple-element.41.b3h, bf16[1,512,256]{2,1,0:T(8,128)(2,1)} %get-tuple-element.42.b3l, ...), custom_call_target="tpu_custom_call" | custom-call | flops 6442450944 | bytes 12582912 | tf_op jit(solution)/shard_map/second/pallas_call | solution.py:229
  261.2 2.3 collective-permute-done.23.refs_2_
  266.0 8.7 %collective-permute-done.28 = f32[2,4,64,256]{3,2,1,0:T(8,128)S(1)} collective-permute-done((f32[2,4,64,256]{3,2,1,0:T(8,128)S(1)}, f32[2,4,64,256]{3,2,1,0:T(8,128)S(1)}, u32[]{:S(2)}, u32[]{:S(2)}) %collective-permute-start.28) | collective-permute-done | bytes 524320 | tf_op jit(solution)/shard_map/ppermute | solution.py:252
  279.6 16.2 %collective-permute-done.43 = f32[2,4,64,256]{3,2,1,0:T(8,128)S(1)} collective-permute-done((f32[2,4,64,256]{3,2,1,0:T(8,128)S(1)}, f32[2,4,64,256]{3,2,1,0:T(8,128)S(1)}, u32[]{:S(2)}, u32[]{:S(2)}) %collective-permute-start.43) | collective-permute-done | bytes 524320 | tf_op jit(solution)/shard_map/ppermute | solution.py:252
  298.0 9.5 %collective-permute-done.29 = f32[4,64,256]{2,1,0:T(8,128)S(1)} collective-permute-done((f32[4,64,256]{2,1,0:T(8,128)S(1)}, f32[4,64,256]{2,1,0:T(8,128)S(1)}, u32[]{:S(2)}, u32[]{:S(2)}) %collective-permute-start.29) | collective-permute-done | bytes 262176 | tf_op jit(solution)/shard_map/ppermute | solution.py:252
  310.8 5.9 %collective-permute-done.44 = f32[4,64,256]{2,1,0:T(8,128)S(1)} collective-permute-done((f32[4,64,256]{2,1,0:T(8,128)S(1)}, f32[4,64,256]{2,1,0:T(8,128)S(1)}, u32[]{:S(2)}, u32[]{:S(2)}) %collective-permute-start.44) | collective-permute-done | bytes 262176 | tf_op jit(solution)/shard_map/ppermute | solution.py:252
  323.6 5.3 %collective-permute-done.39.refs_13_ = f32[4,64,256]{2,1,0:T(8,128)S(1)} collective-permute-done((f32[4,64,256]{2,1,0:T(8,128)S(1)}, f32[4,64,256]{2,1,0:T(8,128)S(1)}, u32[]{:S(2)}, u32[]{:S(2)}) %collective-permute-start.39) | collective-permute-done | bytes 262176 | tf_op jit(solution)/shard_map/ppermute | solution.py:252
  329.6 23.5 %collective-permute-done.32.refs_4_.refs_9_ = f32[2,4,64,256]{3,2,1,0:T(8,128)S(1)} collective-permute-done((f32[2,4,64,256]{3,2,1,0:T(8,128)S(1)}, f32[2,4,64,256]{3,2,1,0:T(8,128)S(1)}, u32[]{:S(2)}, u32[]{:S(2)}) %collective-permute-start.32) | collective-permute-done | bytes 524320 | tf_op jit(solution)/shard_map/ppermute | solution.py:252
  353.2 11.1 %collective-permute-done.47.refs_14_.refs_19_ = f32[2,4,64,256]{3,2,1,0:T(8,128)S(1)} collective-permute-done((f32[2,4,64,256]{3,2,1,0:T(8,128)S(1)}, f32[2,4,64,256]{3,2,1,0:T(8,128)S(1)}, u32[]{:S(2)}, u32[]{:S(2)}) %collective-permute-start.47) | collective-permute-done | bytes 524320 | tf_op jit(solution)/shard_map/ppermute | solution.py:252
  365.1 4.3 %finish.1 = f32[16,4,4096]{2,1,0:T(4,128)} custom-call(f32[2,4,4,64,256]{4,3,2,1,0:T(8,128)} %get-tuple-element.49.refs_0_.refs_5_, f32[2,4,4,64,256]{4,3,2,1,0:T(8,128)} %collective-permute-done.22.refs_1_.refs_6_, f32[2,4,64,256]{3,2,1,0:T(8,128)} %copy-done.13, f32[4,64,256]{2,1,0:T(8,128)} %copy-done.17, f32[2,4,64,256]{3,2,1,0:T(8,128)} %copy-done.11, ...), custom_call_target="tpu_custom_call" | custom-call | tf_op jit(solution)/shard_map/finish/pallas_call | solution.py:292
  (196 shorter events, 67.1 us)
Async XLA Ops:
  7.6 26.1 %collective-permute-start.1 = (f32[3,2,16,512]{3,2,1,0:T(8,128)S(1)}, f32[3,2,16,512]{3,2,1,0:T(8,128)S(1)}, u32[]{:S(2)}, u32[]{:S(2)}) collective-permute-start(f32[3,2,16,512]{3,2,1,0:T(8,128)S(1)} %constant_dynamic-slice_fusion.1), channel_id=1, source_target_pairs={{0,2},{1,3},{2,0},{3,1},{4,6},{5,7},{6,4},{7,5},{8,10},{9,11},{10,... | collective-permute-start | bytes 589832 | tf_op jit(solution)/shard_map/ppermute | solution.py:252
  7.6 26.1 %collective-permute-start = (f32[3,2,16,512]{3,2,1,0:T(8,128)S(1)}, f32[3,2,16,512]{3,2,1,0:T(8,128)S(1)}, u32[]{:S(2)}, u32[]{:S(2)}) collective-permute-start(f32[3,2,16,512]{3,2,1,0:T(8,128)S(1)} %constant_dynamic-slice_fusion.1), channel_id=1, source_target_pairs={{0,1},{1,0},{2,3},{3,2},{4,5},{5,4},{6,7},{7,6},{8,9},{9,8},{10,11... | collective-permute-start | bytes 589832 | tf_op jit(solution)/shard_map/ppermute | solution.py:252
  8.3 28.5 %collective-permute-start.12 = (f32[3,2,16,512]{3,2,1,0:T(8,128)S(1)}, f32[3,2,16,512]{3,2,1,0:T(8,128)S(1)}, u32[]{:S(2)}, u32[]{:S(2)}) collective-permute-start(f32[3,2,16,512]{3,2,1,0:T(8,128)S(1)} %constant_dynamic-slice_fusion), channel_id=1, source_target_pairs={{0,3},{1,2},{2,1},{3,0},{4,7},{5,6},{6,5},{7,4},{8,11},{9,10},{10,... | collective-permute-start | bytes 589832 | tf_op jit(solution)/shard_map/ppermute | solution.py:252
  12.1 29.1 %collective-permute-start.11 = (f32[3,2,16,512]{3,2,1,0:T(8,128)S(1)}, f32[3,2,16,512]{3,2,1,0:T(8,128)S(1)}, u32[]{:S(2)}, u32[]{:S(2)}) collective-permute-start(f32[3,2,16,512]{3,2,1,0:T(8,128)S(1)} %constant_dynamic-slice_fusion), channel_id=1, source_target_pairs={{0,2},{1,3},{2,0},{3,1},{4,6},{5,7},{6,4},{7,5},{8,10},{9,11},{10,... | collective-permute-start | bytes 589832 | tf_op jit(solution)/shard_map/ppermute | solution.py:252
  13.5 27.7 %collective-permute-start.10 = (f32[3,2,16,512]{3,2,1,0:T(8,128)S(1)}, f32[3,2,16,512]{3,2,1,0:T(8,128)S(1)}, u32[]{:S(2)}, u32[]{:S(2)}) collective-permute-start(f32[3,2,16,512]{3,2,1,0:T(8,128)S(1)} %constant_dynamic-slice_fusion), channel_id=1, source_target_pairs={{0,1},{1,0},{2,3},{3,2},{4,5},{5,4},{6,7},{7,6},{8,9},{9,8},{10,11... | collective-permute-start | bytes 589832 | tf_op jit(solution)/shard_map/ppermute | solution.py:252
  42.8 43.7 %collective-permute-start.14 = (f32[3,3,2,16,512]{4,3,2,1,0:T(8,128)S(1)}, f32[3,3,2,16,512]{4,3,2,1,0:T(8,128)}, u32[]{:S(2)}, u32[]{:S(2)}) collective-permute-start(f32[3,3,2,16,512]{4,3,2,1,0:T(8,128)S(1)} %pad_maximum_fusion.1.refs_1_), channel_id=1, source_target_pairs={{0,16},{4,20},{8,24},{12,28},{16,0},{20,4},{24,8},{28,12},{1,17},{... | collective-permute-start | bytes 1769480 | tf_op jit(solution)/shard_map/ppermute | solution.py:252
  44.3 42.2 %collective-permute-start.15 = (f32[3,3,2,16,512]{4,3,2,1,0:T(8,128)S(1)}, f32[3,3,2,16,512]{4,3,2,1,0:T(8,128)}, u32[]{:S(2)}, u32[]{:S(2)}) collective-permute-start(f32[3,3,2,16,512]{4,3,2,1,0:T(8,128)S(1)} %pad_maximum_fusion.1.refs_1_), channel_id=1, source_target_pairs={{0,24},{4,28},{8,16},{12,20},{16,8},{20,12},{24,0},{28,4},{1,25},{... | collective-permute-start | bytes 1769480 | tf_op jit(solution)/shard_map/ppermute | solution.py:252
  50.0 46.0 %collective-permute-start.5 = (f32[3,3,2,16,512]{4,3,2,1,0:T(8,128)S(1)}, f32[3,3,2,16,512]{4,3,2,1,0:T(8,128)S(1)}, u32[]{:S(2)}, u32[]{:S(2)}) collective-permute-start(f32[3,3,2,16,512]{4,3,2,1,0:T(8,128)S(1)} %pad_maximum_fusion.refs_1_), channel_id=1, source_target_pairs={{0,24},{4,28},{8,16},{12,20},{16,8},{20,12},{24,0},{28,4},{1,25},{... | collective-permute-start | bytes 1769480 | tf_op jit(solution)/shard_map/ppermute | solution.py:252
  52.5 43.6 %collective-permute-start.16 = (f32[3,3,2,16,512]{4,3,2,1,0:T(8,128)S(1)}, f32[3,3,2,16,512]{4,3,2,1,0:T(8,128)}, u32[]{:S(2)}, u32[]{:S(2)}) collective-permute-start(f32[3,3,2,16,512]{4,3,2,1,0:T(8,128)S(1)} %pad_maximum_fusion.1.refs_1_), channel_id=1, source_target_pairs={{0,4},{4,0},{8,12},{12,8},{16,20},{20,16},{24,28},{28,24},{1,5},{5... | collective-permute-start | bytes 1769480 | tf_op jit(solution)/shard_map/ppermute | solution.py:252
  62.8 33.8 %collective-permute-start.17 = (f32[3,3,2,16,512]{4,3,2,1,0:T(8,128)}, f32[3,3,2,16,512]{4,3,2,1,0:T(8,128)}, u32[]{:S(2)}, u32[]{:S(2)}) collective-permute-start(f32[3,3,2,16,512]{4,3,2,1,0:T(8,128)} %collective-permute-done.13.refs_2_), channel_id=1, source_target_pairs={{0,4},{4,0},{8,12},{12,8},{16,20},{20,16},{24,28},{28,24},{1,5},{5... | collective-permute-start | bytes 1769480 | tf_op jit(solution)/shard_map/ppermute | solution.py:252
  96.0 41.7 %collective-permute-start.6 = (f32[3,3,2,16,512]{4,3,2,1,0:T(8,128)S(1)}, f32[3,3,2,16,512]{4,3,2,1,0:T(8,128)S(1)}, u32[]{:S(2)}, u32[]{:S(2)}) collective-permute-start(f32[3,3,2,16,512]{4,3,2,1,0:T(8,128)S(1)} %pad_maximum_fusion.refs_1_), channel_id=1, source_target_pairs={{0,4},{4,0},{8,12},{12,8},{16,20},{20,16},{24,28},{28,24},{1,5},{5... | collective-permute-start | bytes 1769480 | tf_op jit(solution)/shard_map/ppermute | solution.py:252
  96.1 44.2 %collective-permute-start.7 = (f32[3,3,2,16,512]{4,3,2,1,0:T(8,128)S(1)}, f32[3,3,2,16,512]{4,3,2,1,0:T(8,128)S(1)}, u32[]{:S(2)}, u32[]{:S(2)}) collective-permute-start(f32[3,3,2,16,512]{4,3,2,1,0:T(8,128)S(1)} %collective-permute-done.3.refs_2_), channel_id=1, source_target_pairs={{0,4},{4,0},{8,12},{12,8},{16,20},{20,16},{24,28},{28,24},{1,5},{5... | collective-permute-start | bytes 1769480 | tf_op jit(solution)/shard_map/ppermute | solution.py:252
  96.6 43.9 %collective-permute-start.8 = (f32[3,3,2,16,512]{4,3,2,1,0:T(8,128)S(1)}, f32[3,3,2,16,512]{4,3,2,1,0:T(8,128)}, u32[]{:S(2)}, u32[]{:S(2)}) collective-permute-start(f32[3,3,2,16,512]{4,3,2,1,0:T(8,128)S(1)} %collective-permute-done.4.refs_3_), channel_id=1, source_target_pairs={{0,4},{4,0},{8,12},{12,8},{16,20},{20,16},{24,28},{28,24},{1,5},{5... | collective-permute-start | bytes 1769480 | tf_op jit(solution)/shard_map/ppermute | solution.py:252
  96.7 45.7 %collective-permute-start.9 = (f32[3,3,2,16,512]{4,3,2,1,0:T(8,128)S(1)}, f32[3,3,2,16,512]{4,3,2,1,0:T(8,128)}, u32[]{:S(2)}, u32[]{:S(2)}) collective-permute-start(f32[3,3,2,16,512]{4,3,2,1,0:T(8,128)S(1)} %collective-permute-done.5.refs_4_), channel_id=1, source_target_pairs={{0,4},{4,0},{8,12},{12,8},{16,20},{20,16},{24,28},{28,24},{1,5},{5... | collective-permute-start | bytes 1769480 | tf_op jit(solution)/shard_map/ppermute | solution.py:252
  137.7 26.2 %collective-permute-start.21 = (f32[2,2,2,32,512]{4,3,2,1,0:T(8,128)}, f32[2,2,2,32,512]{4,3,2,1,0:T(8,128)S(1)}, u32[]{:S(2)}, u32[]{:S(2)}) collective-permute-start(f32[2,2,2,32,512]{4,3,2,1,0:T(8,128)} %get-tuple-element.48), channel_id=1, source_target_pairs={{0,1},{1,0},{2,3},{3,2},{4,5},{5,4},{6,7},{7,6},{8,9},{9,8},{10,11... | collective-permute-start | bytes 1572872 | tf_op jit(solution)/shard_map/ppermute | solution.py:252
  140.4 37.0 %collective-permute-start.25 = (f32[2,2,2,32,512]{4,3,2,1,0:T(8,128)}, f32[2,2,2,32,512]{4,3,2,1,0:T(8,128)}, u32[]{:S(2)}, u32[]{:S(2)}) collective-permute-start(f32[2,2,2,32,512]{4,3,2,1,0:T(8,128)} %get-tuple-element.53), channel_id=1, source_target_pairs={{0,1},{1,0},{2,3},{3,2},{4,5},{5,4},{6,7},{7,6},{8,9},{9,8},{10,11... | collective-permute-start | bytes 1572872 | tf_op jit(solution)/shard_map/ppermute | solution.py:252
  140.5 46.0 %collective-permute-start.26 = (f32[2,2,2,32,512]{4,3,2,1,0:T(8,128)}, f32[2,2,2,32,512]{4,3,2,1,0:T(8,128)}, u32[]{:S(2)}, u32[]{:S(2)}) collective-permute-start(f32[2,2,2,32,512]{4,3,2,1,0:T(8,128)} %get-tuple-element.54), channel_id=1, source_target_pairs={{0,1},{1,0},{2,3},{3,2},{4,5},{5,4},{6,7},{7,6},{8,9},{9,8},{10,11... | collective-permute-start | bytes 1572872 | tf_op jit(solution)/shard_map/ppermute | solution.py:252
  142.4 57.0 %collective-permute-start.35 = (f32[2,2,2,32,512]{4,3,2,1,0:T(8,128)}, f32[2,2,2,32,512]{4,3,2,1,0:T(8,128)S(1)}, u32[]{:S(2)}, u32[]{:S(2)}) collective-permute-start(f32[2,2,2,32,512]{4,3,2,1,0:T(8,128)} %get-tuple-element.59), channel_id=1, source_target_pairs={{0,1},{1,0},{2,3},{3,2},{4,5},{5,4},{6,7},{7,6},{8,9},{9,8},{10,11... | collective-permute-start | bytes 1572872 | tf_op jit(solution)/shard_map/ppermute | solution.py:252
  153.6 55.2 %collective-permute-start.36 = (f32[2,2,2,32,512]{4,3,2,1,0:T(8,128)S(1)}, f32[2,2,2,32,512]{4,3,2,1,0:T(8,128)S(1)}, u32[]{:S(2)}, u32[]{:S(2)}) collective-permute-start(f32[2,2,2,32,512]{4,3,2,1,0:T(8,128)S(1)} %copy-done.26), channel_id=1, source_target_pairs={{0,1},{1,0},{2,3},{3,2},{4,5},{5,4},{6,7},{7,6},{8,9},{9,8},{10,11... | collective-permute-start | bytes 1572872 | tf_op jit(solution)/shard_map/ppermute | solution.py:252
  163.9 58.5 %collective-permute-start.40 = (f32[2,2,2,32,512]{4,3,2,1,0:T(8,128)S(1)}, f32[2,2,2,32,512]{4,3,2,1,0:T(8,128)S(1)}, u32[]{:S(2)}, u32[]{:S(2)}) collective-permute-start(f32[2,2,2,32,512]{4,3,2,1,0:T(8,128)S(1)} %copy-done.24), channel_id=1, source_target_pairs={{0,1},{1,0},{2,3},{3,2},{4,5},{5,4},{6,7},{7,6},{8,9},{9,8},{10,11... | collective-permute-start | bytes 1572872 | tf_op jit(solution)/shard_map/ppermute | solution.py:252
  177.4 53.1 %collective-permute-start.41 = (f32[2,2,2,32,512]{4,3,2,1,0:T(8,128)S(1)}, f32[2,2,2,32,512]{4,3,2,1,0:T(8,128)S(1)}, u32[]{:S(2)}, u32[]{:S(2)}) collective-permute-start(f32[2,2,2,32,512]{4,3,2,1,0:T(8,128)S(1)} %copy-done.25), channel_id=1, source_target_pairs={{0,1},{1,0},{2,3},{3,2},{4,5},{5,4},{6,7},{7,6},{8,9},{9,8},{10,11... | collective-permute-start | bytes 1572872 | tf_op jit(solution)/shard_map/ppermute | solution.py:252
  186.5 61.0 %collective-permute-start.22 = (f32[2,4,4,64,256]{4,3,2,1,0:T(8,128)}, f32[2,4,4,64,256]{4,3,2,1,0:T(8,128)}, u32[]{:S(2)}, u32[]{:S(2)}) collective-permute-start(f32[2,4,4,64,256]{4,3,2,1,0:T(8,128)} %get-tuple-element.50), channel_id=1, source_target_pairs={{0,4},{4,0},{8,12},{12,8},{16,20},{20,16},{24,28},{28,24},{1,5},{5... | collective-permute-start | bytes 6291464 | tf_op jit(solution)/shard_map/ppermute | solution.py:252
  199.4 50.8 %collective-permute-start.27 = (f32[2,4,4,64,256]{4,3,2,1,0:T(8,128)}, f32[2,4,4,64,256]{4,3,2,1,0:T(8,128)}, u32[]{:S(2)}, u32[]{:S(2)}) collective-permute-start(f32[2,4,4,64,256]{4,3,2,1,0:T(8,128)} %get-tuple-element.56), channel_id=1, source_target_pairs={{0,4},{4,0},{8,12},{12,8},{16,20},{20,16},{24,28},{28,24},{1,5},{5... | collective-permute-start | bytes 6291464 | tf_op jit(solution)/shard_map/ppermute | solution.py:252
  222.4 32.5 %collective-permute-start.37 = (f32[2,4,4,64,256]{4,3,2,1,0:T(8,128)}, f32[2,4,4,64,256]{4,3,2,1,0:T(8,128)}, u32[]{:S(2)}, u32[]{:S(2)}) collective-permute-start(f32[2,4,4,64,256]{4,3,2,1,0:T(8,128)} %get-tuple-element.62), channel_id=1, source_target_pairs={{0,4},{4,0},{8,12},{12,8},{16,20},{20,16},{24,28},{28,24},{1,5},{5... | collective-permute-start | bytes 6291464 | tf_op jit(solution)/shard_map/ppermute | solution.py:252
  254.9 24.5 %collective-permute-start.33 = (f32[2,4,64,256]{3,2,1,0:T(8,128)S(1)}, f32[2,4,64,256]{3,2,1,0:T(8,128)S(1)}, u32[]{:S(2)}, u32[]{:S(2)}) collective-permute-start(f32[2,4,64,256]{3,2,1,0:T(8,128)S(1)} %fusion.7), channel_id=1, source_target_pairs={{0,8},{4,12},{8,0},{12,4},{16,24},{20,28},{24,16},{28,20},{1,9},{5... | collective-permute-start | bytes 1572872 | tf_op jit(solution)/shard_map/ppermute | solution.py:252
  258.0 61.5 %collective-permute-start.38 = (f32[2,4,64,256]{3,2,1,0:T(8,128)S(1)}, f32[2,4,64,256]{3,2,1,0:T(8,128)S(1)}, u32[]{:S(2)}, u32[]{:S(2)}) collective-permute-start(f32[2,4,64,256]{3,2,1,0:T(8,128)S(1)} %fusion.5), channel_id=1, source_target_pairs={{0,16},{4,20},{8,24},{12,28},{16,0},{20,4},{24,8},{28,12},{1,17},{... | collective-permute-start | bytes 1572872 | tf_op jit(solution)/shard_map/ppermute | solution.py:252
  263.5 32.2 %collective-permute-start.43 = (f32[2,4,64,256]{3,2,1,0:T(8,128)S(1)}, f32[2,4,64,256]{3,2,1,0:T(8,128)S(1)}, u32[]{:S(2)}, u32[]{:S(2)}) collective-permute-start(f32[2,4,64,256]{3,2,1,0:T(8,128)S(1)} %fusion.4), channel_id=1, source_target_pairs={{0,16},{4,20},{8,24},{12,28},{16,0},{20,4},{24,8},{28,12},{1,17},{... | collective-permute-start | bytes 1572872 | tf_op jit(solution)/shard_map/ppermute | solution.py:252
  275.8 46.6 %collective-permute-start.48 = (f32[2,4,64,256]{3,2,1,0:T(8,128)S(1)}, f32[2,4,64,256]{3,2,1,0:T(8,128)S(1)}, u32[]{:S(2)}, u32[]{:S(2)}) collective-permute-start(f32[2,4,64,256]{3,2,1,0:T(8,128)S(1)} %fusion.1), channel_id=1, source_target_pairs={{0,8},{4,12},{8,0},{12,4},{16,24},{20,28},{24,16},{28,20},{1,9},{5... | collective-permute-start | bytes 1572872 | tf_op jit(solution)/shard_map/ppermute | solution.py:252
  279.4 28.1 %collective-permute-start.29 = (f32[4,64,256]{2,1,0:T(8,128)S(1)}, f32[4,64,256]{2,1,0:T(8,128)S(1)}, u32[]{:S(2)}, u32[]{:S(2)}) collective-permute-start(f32[4,64,256]{2,1,0:T(8,128)S(1)} %fusion.59), channel_id=1, source_target_pairs={{0,8},{4,12},{8,0},{12,4},{16,24},{20,28},{24,16},{28,20},{1,9},{5... | collective-permute-start | bytes 786440 | tf_op jit(solution)/shard_map/ppermute | solution.py:252
  297.3 25.9 %collective-permute-start.24 = (f32[4,64,256]{2,1,0:T(8,128)S(1)}, f32[4,64,256]{2,1,0:T(8,128)S(1)}, u32[]{:S(2)}, u32[]{:S(2)}) collective-permute-start(f32[4,64,256]{2,1,0:T(8,128)S(1)} %fusion.65), channel_id=1, source_target_pairs={{0,8},{4,12},{8,0},{12,4},{16,24},{20,28},{24,16},{28,20},{1,9},{5... | collective-permute-start | bytes 786440 | tf_op jit(solution)/shard_map/ppermute | solution.py:252
  318.2 34.9 %collective-permute-start.32 = (f32[2,4,64,256]{3,2,1,0:T(8,128)S(1)}, f32[2,4,64,256]{3,2,1,0:T(8,128)S(1)}, u32[]{:S(2)}, u32[]{:S(2)}) collective-permute-start(f32[2,4,64,256]{3,2,1,0:T(8,128)S(1)} %pad_maximum_fusion.2), channel_id=1, source_target_pairs={{0,2},{1,3},{2,0},{3,1},{4,6},{5,7},{6,4},{7,5},{8,10},{9,11},{10,... | collective-permute-start | bytes 1572872 | tf_op jit(solution)/shard_map/ppermute | solution.py:252
  319.5 44.8 %collective-permute-start.47 = (f32[2,4,64,256]{3,2,1,0:T(8,128)S(1)}, f32[2,4,64,256]{3,2,1,0:T(8,128)S(1)}, u32[]{:S(2)}, u32[]{:S(2)}) collective-permute-start(f32[2,4,64,256]{3,2,1,0:T(8,128)S(1)} %pad_maximum_fusion.3), channel_id=1, source_target_pairs={{0,2},{1,3},{2,0},{3,1},{4,6},{5,7},{6,4},{7,5},{8,10},{9,11},{10,... | collective-permute-start | bytes 1572872 | tf_op jit(solution)/shard_map/ppermute | solution.py:252
  (51 other events, 931.4 us)
